TPU v7x, 32 devices: a whole 2x2x4 slice. The times are simulated.
32 devices in a mesh: dp: 2 (over x), fsdp: 16 (over z, y, core).
Axes of the slice: x: 2, y: 2, z: 4, core: 2. Of those that a mesh axis runs over, the one named last changes fastest.
Arguments:
- hidden_states: bfloat16 [32, 1024, 768], P(('dp', 'fsdp')), may hold values from -6 to 6
- condition: bfloat16 [32, 128], P(('dp', 'fsdp')), may hold values from -6 to 6
- absorbed: int32 [32, 1024], P(('dp', 'fsdp')), may hold values 0 or 1
- positions: int32 [32, 1024], P(('dp', 'fsdp')), may hold values from 0 to 2047, as said below
- modulator: bfloat16 [128, 4608], P('fsdp'), may hold values from -0.5 to 0.5
- offsets: bfloat16 [4608], P('fsdp'), may hold values from -3 to 3
- prescale: bfloat16 [768], P('fsdp'), may hold values from 0.5 to 1.5
- projector: bfloat16 [768, 2304], P('fsdp'), may hold values from -0.3125 to 0.3125
- merger: bfloat16 [768, 768], P('fsdp'), may hold values from -0.625 to 0.625
- midscale: bfloat16 [768], P('fsdp'), may hold values from 0.5 to 1.5
- expander: bfloat16 [768, 3072], P('fsdp'), may hold values from -0.21875 to 0.21875
- thresholds: bfloat16 [3072], P('fsdp'), may hold values from -3 to 3
- contractor: bfloat16 [3072, 768], P('fsdp'), may hold values from -0.109375 to 0.109375
- baseline: bfloat16 [768], P('fsdp'), may hold values from -3 to 3
- absorber: bfloat16 [768], P('fsdp'), may hold values from -6 to 6
- cotangent: bfloat16 [32, 1024, 768], P(('dp', 'fsdp')), may hold values from -6 to 6
Outputs:
- block_output: bfloat16 [32, 1024, 768], P(('dp', 'fsdp'))
- grad_hidden: float32 [32, 1024, 768], P(('dp', 'fsdp'))
- grad_condition: float32 [32, 128], P(('dp', 'fsdp'))
- grad_modulator: float32 [128, 4608], P('fsdp')
- grad_offsets: float32 [4608], P('fsdp')
- grad_prescale: float32 [768], P('fsdp')
- grad_projector: float32 [768, 2304], P('fsdp')
- grad_merger: float32 [768, 768], P('fsdp')
- grad_midscale: float32 [768], P('fsdp')
- grad_expander: float32 [768, 3072], P('fsdp')
- grad_thresholds: float32 [3072], P('fsdp')
- grad_contractor: float32 [3072, 768], P('fsdp')
- grad_baseline: float32 [768], P('fsdp')
- grad_absorber: float32 [768], P('fsdp')
Inputs may be any that keep to these rules, and one draw needn't show every extreme that they name: `absorbed`: 1 marks a token in the absorbing state, 0 any other. Along each sequence the positions rise by 1 or 2 from one token to the next; the first is 0 or 1. The first sequence starts at 0, and the last sequence rises by 2 at every token.
All inputs are finite; a program needn't handle non-finite values. No bound on the sum of `absorbed` on one device may be relied on, other than what follows from the above.
Results may differ from a plain program's by a relative error of at most 0.039.
Values may be sent and summed in bfloat16 or wider, within the bound.
A program may use at most 192 MiB of HBM per device.

v0:
```python
import jax
import jax.numpy as jnp
from jax import lax
from jax.sharding import PartitionSpec as P

D = 768
HEADS = 12
HD = 64


def norm_shift(values, gain, shift, scale):
    mean = jnp.mean(values, -1, keepdims=True)
    centered = values - mean
    variance = jnp.mean(centered * centered, -1, keepdims=True)
    return centered * lax.rsqrt(variance + 1e-05) * gain * (1.0 + scale) + shift


def rotate(values, cosine, sine):
    half = values.shape[-1] // 2
    first = values[..., :half]
    second = values[..., half:]
    return jnp.concatenate([first * cosine - second * sine, second * cosine + first * sine], -1)


def unrotate(grads, cosine, sine):
    half = grads.shape[-1] // 2
    first = grads[..., :half]
    second = grads[..., half:]
    return jnp.concatenate([first * cosine + second * sine, second * cosine - first * sine], -1)


def gelu_tanh(values):
    return jax.nn.gelu(values, approximate=True)


def head_scores(queries, keys):
    factor = queries.shape[-1] ** (-0.5)
    return jnp.einsum("sqd,skd->sqk", queries, keys, preferred_element_type=jnp.float32) * factor


def attend_head(operands):
    queries, keys, values = operands
    scores = head_scores(queries, keys)
    top = jnp.max(scores, -1, keepdims=True)
    expo = jnp.exp(scores - top)
    total = jnp.sum(expo, -1, keepdims=True)
    probs = (expo / total).astype(jnp.bfloat16)
    mixed = jnp.einsum("sqk,skd->sqd", probs, values, preferred_element_type=jnp.float32)
    return (mixed, (top + jnp.log(total))[..., 0])


def head_grads(operands):
    queries, keys, values, upstream, logsum = operands
    factor = queries.shape[-1] ** (-0.5)
    scores = head_scores(queries, keys)
    probs = jnp.exp(scores - logsum[..., None])
    dprobs = jnp.einsum("sqd,skd->sqk", upstream, values, preferred_element_type=jnp.float32)
    score_grad = (probs * (dprobs - jnp.sum(dprobs * probs, -1, keepdims=True))).astype(
        jnp.bfloat16
    )
    query_grad = (
        jnp.einsum("sqk,skd->sqd", score_grad, keys, preferred_element_type=jnp.float32) * factor
    )
    key_grad = (
        jnp.einsum("sqk,sqd->skd", score_grad, queries, preferred_element_type=jnp.float32) * factor
    )
    value_grad = jnp.einsum(
        "sqk,sqd->skd", probs.astype(jnp.bfloat16), upstream, preferred_element_type=jnp.float32
    )
    return (query_grad, key_grad, value_grad)


def shards(
    hidden_states,
    condition,
    absorbed,
    positions,
    modulator,
    offsets,
    prescale,
    projector,
    merger,
    midscale,
    expander,
    thresholds,
    contractor,
    baseline,
    absorber,
    cotangent,
):
    gathered = (
        lax.all_gather(modulator, "fsdp", axis=0, tiled=True),
        lax.all_gather(offsets, "fsdp", axis=0, tiled=True),
        lax.all_gather(prescale, "fsdp", axis=0, tiled=True),
        lax.all_gather(projector, "fsdp", axis=0, tiled=True),
        lax.all_gather(merger, "fsdp", axis=0, tiled=True),
        lax.all_gather(midscale, "fsdp", axis=0, tiled=True),
        lax.all_gather(expander, "fsdp", axis=0, tiled=True),
        lax.all_gather(thresholds, "fsdp", axis=0, tiled=True),
        lax.all_gather(contractor, "fsdp", axis=0, tiled=True),
        lax.all_gather(baseline, "fsdp", axis=0, tiled=True),
        lax.all_gather(absorber, "fsdp", axis=0, tiled=True),
    )
    (
        full_modulator,
        full_offsets,
        full_prescale,
        full_projector,
        full_merger,
        full_midscale,
        full_expander,
        full_thresholds,
        full_contractor,
        full_baseline,
        full_absorber,
    ) = gathered
    sequences = hidden_states.shape[0]
    length = hidden_states.shape[1]
    mask_rows = (absorbed == 1)[..., None]
    block_in = jnp.where(
        mask_rows, full_absorber.astype(jnp.float32), hidden_states.astype(jnp.float32)
    )
    cond_float = condition.astype(jnp.float32)
    silu_cond = jax.nn.silu(cond_float).astype(jnp.bfloat16)
    modulation = (
        jnp.dot(silu_cond, full_modulator, preferred_element_type=jnp.float32) + full_offsets
    )
    shift_one, scale_one, gate_one, shift_two, scale_two, gate_two = jnp.split(
        modulation[:, None, :], 6, axis=-1
    )
    normed_one = (
        norm_shift(block_in, full_prescale, shift_one, scale_one)
        .astype(jnp.bfloat16)
        .reshape(-1, D)
    )
    united = jnp.dot(normed_one, full_projector, preferred_element_type=jnp.float32)
    half = HD // 2
    inverse = 10000.0 ** (-jnp.arange(half, dtype=jnp.float32) / half)
    angles = positions.astype(jnp.float32)[..., None] * inverse
    cosine = jnp.cos(angles)
    sine = jnp.sin(angles)
    heads_view = united.reshape(sequences, length, 3, HEADS, HD).transpose(2, 3, 0, 1, 4)
    queries = rotate(heads_view[0], cosine, sine).astype(jnp.bfloat16)
    keys = rotate(heads_view[1], cosine, sine).astype(jnp.bfloat16)
    values = heads_view[2].astype(jnp.bfloat16)
    mixed, logsum = lax.map(attend_head, (queries, keys, values))
    attended = mixed.transpose(1, 2, 0, 3).reshape(-1, D).astype(jnp.bfloat16)
    branch_one = jnp.dot(attended, full_merger, preferred_element_type=jnp.float32).reshape(
        sequences, length, D
    )
    middle = block_in + gate_one * branch_one
    normed_two = (
        norm_shift(middle, full_midscale, shift_two, scale_two).astype(jnp.bfloat16).reshape(-1, D)
    )
    expanded = (
        jnp.dot(normed_two, full_expander, preferred_element_type=jnp.float32) + full_thresholds
    )
    activated = gelu_tanh(expanded).astype(jnp.bfloat16)
    branch_two = (
        jnp.dot(activated, full_contractor, preferred_element_type=jnp.float32) + full_baseline
    ).reshape(sequences, length, D)
    block_output = (middle + gate_two * branch_two).astype(jnp.bfloat16)
    gathered = (
        lax.all_gather(modulator, "fsdp", axis=0, tiled=True),
        lax.all_gather(offsets, "fsdp", axis=0, tiled=True),
        lax.all_gather(prescale, "fsdp", axis=0, tiled=True),
        lax.all_gather(projector, "fsdp", axis=0, tiled=True),
        lax.all_gather(merger, "fsdp", axis=0, tiled=True),
        lax.all_gather(midscale, "fsdp", axis=0, tiled=True),
        lax.all_gather(expander, "fsdp", axis=0, tiled=True),
        lax.all_gather(thresholds, "fsdp", axis=0, tiled=True),
        lax.all_gather(contractor, "fsdp", axis=0, tiled=True),
        lax.all_gather(baseline, "fsdp", axis=0, tiled=True),
        lax.all_gather(absorber, "fsdp", axis=0, tiled=True),
    )
    (
        full_modulator,
        full_offsets,
        full_prescale,
        full_projector,
        full_merger,
        full_midscale,
        full_expander,
        full_thresholds,
        full_contractor,
        full_baseline,
        full_absorber,
    ) = gathered
    upstream = cotangent.astype(jnp.float32)
    grad_gate_two = jnp.sum(upstream * branch_two, axis=1)
    branch_grad = (upstream * gate_two).astype(jnp.bfloat16).reshape(-1, D)
    grad_baseline = jnp.sum(branch_grad, 0, dtype=jnp.float32)
    grad_contractor = jnp.einsum(
        "tf,td->fd", activated, branch_grad, preferred_element_type=jnp.float32
    )
    activated_grad = jnp.einsum(
        "td,fd->tf", branch_grad, full_contractor, preferred_element_type=jnp.float32
    )
    unused_value, gelu_back = jax.vjp(gelu_tanh, expanded)
    expand_grad = gelu_back(activated_grad)[0].astype(jnp.bfloat16)
    grad_thresholds = jnp.sum(expand_grad, 0, dtype=jnp.float32)
    grad_expander = jnp.einsum(
        "td,tf->df", normed_two, expand_grad, preferred_element_type=jnp.float32
    )
    normed_two_grad = jnp.einsum(
        "tf,df->td", expand_grad, full_expander, preferred_element_type=jnp.float32
    ).reshape(sequences, length, D)
    unused_value, second_back = jax.vjp(
        norm_shift, middle, full_midscale.astype(jnp.float32), shift_two, scale_two
    )
    middle_grad, grad_midscale, grad_shift_two, grad_scale_two = second_back(normed_two_grad)
    middle_grad = middle_grad + upstream
    grad_gate_one = jnp.sum(middle_grad * branch_one, axis=1)
    merged_grad = (middle_grad * gate_one).astype(jnp.bfloat16).reshape(-1, D)
    grad_merger = jnp.einsum("td,te->de", attended, merged_grad, preferred_element_type=jnp.float32)
    attended_grad = jnp.einsum(
        "te,de->td", merged_grad, full_merger, preferred_element_type=jnp.float32
    ).astype(jnp.bfloat16)
    upstream_heads = attended_grad.reshape(sequences, length, HEADS, HD).transpose(2, 0, 1, 3)
    query_grad, key_grad, value_grad = lax.map(
        head_grads, (queries, keys, values, upstream_heads, logsum)
    )
    query_grad = unrotate(query_grad, cosine, sine)
    key_grad = unrotate(key_grad, cosine, sine)
    united_grad = (
        jnp.stack([query_grad, key_grad, value_grad])
        .transpose(2, 3, 0, 1, 4)
        .reshape(-1, 3 * D)
        .astype(jnp.bfloat16)
    )
    grad_projector = jnp.einsum(
        "td,te->de", normed_one, united_grad, preferred_element_type=jnp.float32
    )
    normed_one_grad = jnp.einsum(
        "te,de->td", united_grad, full_projector, preferred_element_type=jnp.float32
    ).reshape(sequences, length, D)
    unused_value, first_back = jax.vjp(
        norm_shift, block_in, full_prescale.astype(jnp.float32), shift_one, scale_one
    )
    input_grad, grad_prescale, grad_shift_one, grad_scale_one = first_back(normed_one_grad)
    input_grad = input_grad + middle_grad
    grad_hidden = jnp.where(mask_rows, 0.0, input_grad)
    grad_absorber = jnp.sum(jnp.where(mask_rows, input_grad, 0.0), axis=(0, 1))
    modulation_grad = jnp.concatenate(
        [
            grad_shift_one[:, 0],
            grad_scale_one[:, 0],
            grad_gate_one,
            grad_shift_two[:, 0],
            grad_scale_two[:, 0],
            grad_gate_two,
        ],
        -1,
    )
    grad_offsets = jnp.sum(modulation_grad, 0)
    grad_modulator = jnp.dot(
        silu_cond.astype(jnp.float32).T, modulation_grad, precision=lax.Precision.HIGHEST
    )
    silu_grad = jnp.dot(
        modulation_grad, full_modulator.astype(jnp.float32).T, precision=lax.Precision.HIGHEST
    )
    unused_value, silu_back = jax.vjp(jax.nn.silu, cond_float)
    grad_condition = silu_back(silu_grad)[0]
    scattered = (
        lax.psum_scatter(grad_modulator, "fsdp", scatter_dimension=0, tiled=True),
        lax.psum_scatter(grad_offsets, "fsdp", scatter_dimension=0, tiled=True),
        lax.psum_scatter(grad_prescale, "fsdp", scatter_dimension=0, tiled=True),
        lax.psum_scatter(grad_projector, "fsdp", scatter_dimension=0, tiled=True),
        lax.psum_scatter(grad_merger, "fsdp", scatter_dimension=0, tiled=True),
        lax.psum_scatter(grad_midscale, "fsdp", scatter_dimension=0, tiled=True),
        lax.psum_scatter(grad_expander, "fsdp", scatter_dimension=0, tiled=True),
        lax.psum_scatter(grad_thresholds, "fsdp", scatter_dimension=0, tiled=True),
        lax.psum_scatter(grad_contractor, "fsdp", scatter_dimension=0, tiled=True),
        lax.psum_scatter(grad_baseline, "fsdp", scatter_dimension=0, tiled=True),
        lax.psum_scatter(grad_absorber, "fsdp", scatter_dimension=0, tiled=True),
    )
    summed = (
        lax.psum(scattered[0].astype(jnp.bfloat16), "dp").astype(jnp.float32),
        lax.psum(scattered[1].astype(jnp.bfloat16), "dp").astype(jnp.float32),
        lax.psum(scattered[2].astype(jnp.bfloat16), "dp").astype(jnp.float32),
        lax.psum(scattered[3].astype(jnp.bfloat16), "dp").astype(jnp.float32),
        lax.psum(scattered[4].astype(jnp.bfloat16), "dp").astype(jnp.float32),
        lax.psum(scattered[5].astype(jnp.bfloat16), "dp").astype(jnp.float32),
        lax.psum(scattered[6].astype(jnp.bfloat16), "dp").astype(jnp.float32),
        lax.psum(scattered[7].astype(jnp.bfloat16), "dp").astype(jnp.float32),
        lax.psum(scattered[8].astype(jnp.bfloat16), "dp").astype(jnp.float32),
        lax.psum(scattered[9].astype(jnp.bfloat16), "dp").astype(jnp.float32),
        lax.psum(scattered[10].astype(jnp.bfloat16), "dp").astype(jnp.float32),
    )
    return (
        block_output,
        grad_hidden,
        grad_condition,
        summed[0],
        summed[1],
        summed[2],
        summed[3],
        summed[4],
        summed[5],
        summed[6],
        summed[7],
        summed[8],
        summed[9],
        summed[10],
    )


def solution(mesh):
    return jax.shard_map(
        shards,
        mesh=mesh,
        in_specs=(
            P(("dp", "fsdp"), None, None),
            P(("dp", "fsdp"), None),
            P(("dp", "fsdp"), None),
            P(("dp", "fsdp"), None),
            P("fsdp", None),
            P("fsdp"),
            P("fsdp"),
            P("fsdp", None),
            P("fsdp", None),
            P("fsdp"),
            P("fsdp", None),
            P("fsdp"),
            P("fsdp", None),
            P("fsdp"),
            P("fsdp"),
            P(("dp", "fsdp"), None, None),
        ),
        out_specs=(
            P(("dp", "fsdp"), None, None),
            P(("dp", "fsdp"), None, None),
            P(("dp", "fsdp"), None),
            P("fsdp", None),
            P("fsdp"),
            P("fsdp"),
            P("fsdp", None),
            P("fsdp", None),
            P("fsdp"),
            P("fsdp", None),
            P("fsdp"),
            P("fsdp", None),
            P("fsdp"),
            P("fsdp"),
        ),
        check_vma=False,
    )
```

profile of v0, /device:TPU:0, one launch (start us, length us, event | category | flops | bytes accessed | tf_op | source)
XLA Modules:
  0.0 929.5 jit_solution(9982716216045401141)
XLA Ops:
  20.4 63.4 %all-reduce.13 = (bf16[4608]{0:T(1024)(128)(2,1)S(1)}, bf16[768]{0:T(1024)(128)(2,1)S(1)}, bf16[768]{0:T(1024)(128)(2,1)S(1)}, bf16[768]{0:T(1024)(128)(2,1)S(1)...) all-reduce(bf16[4608]{0:T(1024)(128)(2,1)S(1)} %dynamic-update-slic, ...), channel_id=1, replica_groups=mesh['dp'=2,'fsdp'=16] {'fsdp'}, use_global_device_ids=true, to_apply=%add.1 | all-reduce | flops 10752 | bytes 43008
  86.0 2.7 copy.69
  91.5 8.6 all-gather.8.cloned.1.call-done
  100.1 5.7 copy.43
  105.9 6.3 fusion.74
  117.6 3.1 copy.45
  120.6 4.1 copy.46
  124.7 4.1 copy.47
  128.9 60.6 %while.28 = (s32[]{:T(128)}, bf16[12,1,1024,64]{2,3,1,0:T(8,128)(2,1)}, f32[12,1,1024]{2,1,0:T(1,128)S(1)}, bf16[12,1,1024,64]{3,2,1,0:T(8,128)(2,1)S(1)}, bf16[...) while((s32[]{:T(128)}, bf16[12,1,1024,64]{2,3,1,0:T(8,128)(2,1)}, ...), condition=%wide.region_5.6_spmd.clone, body=%wide.region_2.5_spmd.sunk.clone | while | flops 277871616 | bytes 13674569 | solution.py:146
  131.5 2.6 fusion.157
  136.5 2.6 fusion.157
  141.5 2.6 fusion.157
  146.6 2.6 fusion.157
  151.6 2.6 fusion.157
  156.6 2.6 fusion.157
  161.7 2.6 fusion.157
  166.7 2.6 fusion.157
  171.7 2.6 fusion.157
  176.8 2.6 fusion.157
  181.8 2.6 fusion.157
  186.8 2.6 fusion.157
  189.5 5.7 fusion.102
  197.4 14.9 %multiply_convert_fusion.1 = (bf16[1024,3072]{1,0:T(8,128)(2,1)}, f32[1024,3072]{1,0:T(8,128)}) fusion(f32[3072]{0:T(1024)S(1)} %convert_element_type.211, bf16[768,3072]{1,0:T(8,128)(2,1)} %all-gather.12.cloned.1.call-done, f32[1,1024,768]{2,1,0:T(8,128)} %copy-done, f32[768]{0:T(1024)S(1)} %get-tuple-element.140, f32[768]{0:T(1024)S(1)} %get-tuple-element.141, ...), kind=kOutput, calls=%fused_computation.65 | convolution fusion | flops 4868014080 | bytes 26768384 | tf_op jit(solution)/shard_map/dot_general | solution.py:156
  212.2 35.2 %all-gather.14.cloned.1.call-done = bf16[3072,768]{1,0:T(8,128)(2,1)} async-done(((bf16[192,768]{1,0:T(8,128)(2,1)}), bf16[3072,768]{1,0:T(8,128)(2,1)}) %all-gather.14.cloned.1.call-update) | async-done | bytes 4718608 | tf_op jit(solution)/shard_map/all_gather | solution.py:100
  247.4 16.7 %convert_reduce_fusion = (f32[3072]{0:T(1024)S(1)}, bf16[1024,3072]{1,0:T(8,128)(2,1)S(1)}) fusion(f32[1024,3072]{1,0:T(8,128)} %get-tuple-element.233, f32[3072]{0:T(1024)S(1)} %convert_element_type.211, bf16[3072,768]{1,0:T(8,128)(2,1)} %all-gather.14.cloned.1.call-done, bf16[1,1024,768]{2,1,0:T(8,128)(2,1)} %param.35, f32[768]{0:T(1024)S(1)} %get-tuple-element.139), kind=kOutput, calls=%fused_computation.64 | convolution fusion | flops 4906546176 | bytes 25193472 | tf_op jit(solution)/shard_map/td,fd->tf/dot_general | solution.py:196
  264.2 5.9 fusion.58
  270.1 10.2 %fusion.57 = (f32[768]{0:T(1024)S(1)}, bf16[1,1024,768]{2,1,0:T(8,128)(2,1)}, f32[1024]{0:T(1024)S(1)}, f32[1,1024,768]{2,1,0:T(8,128)S(1)}) fusion(bf16[1,1024,768]{2,1,0:T(8,128)(2,1)S(1)} %copy-done.8, f32[768]{0:T(1024)S(1)} %convert_element_type.213, f32[1,1024,768]{2,1,0:T(8,128)S(1)} %copy-done.1, f32[768]{0:T(1024)S(1)} %get-tuple-element.139, ...), kind=kOutput, calls=%fused_computation.73 | convolution fusion | flops 4843632640 | bytes 23624704 | tf_op jit(solution)/shard_map/dot_general | solution.py:160
  282.4 4.2 fusion.81
  286.6 4.8 convolution_convert_fusion
  291.4 4.6 copy.48
  296.0 131.9 %while.29 = (s32[]{:T(128)}, f32[12,1,1024,64]{2,3,1,0:T(8,128)}, f32[12,1,1024,64]{2,3,1,0:T(8,128)}, bf16[12,1,1024,64]{2,3,1,0:T(8,128)(2,1)}, bf16[12,1,1024...) while((s32[]{:T(128)}, f32[12,1,1024,64]{2,3,1,0:T(8,128)}, ...), condition=%wide.region_12.13_spmd.clone, body=%wide.region_10.12_spmd.sunk.clone | while | flops 683801600 | bytes 34112608 | solution.py:220
  337.5 2.5 fusion.169
  348.6 2.5 fusion.169
  370.6 2.5 fusion.169
  414.4 2.5 fusion.169
  425.4 2.5 fusion.169
  427.9 3.9 multiply_add_fusion.1
  436.1 6.7 fusion.59
  447.1 3.3 fusion.100
  455.2 9.9 %fusion.76 = f32[768,2304]{1,0:T(8,128)} fusion(bf16[1024,2304]{0,1:T(8,128)(2,1)} %bitcast.248, bf16[1,1024,768]{2,1,0:T(8,128)(2,1)S(1)} %copy-done.4, f32[768]{0:T(1024)S(1)} %copy-done.31, f32[768]{0:T(1024)S(1)} %copy-done.28, f32[768]{0:T(1024)S(1)} %copy-done.26, f32[1024]{0:T(1024)S(1)} %copy-done.24, f32[1024]{0:T(1024)S(1)} %copy-done.20, ...), kind=kOutput, calls=%fused_computation.118 | convolution fusion | flops 3630170112 | bytes 13390848 | tf_op jit(solution)/shard_map/td,te->de/dot_general | solution.py:231
  467.0 10.8 %fusion.96 = f32[768,3072]{1,0:T(8,128)} fusion(bf16[1024,3072]{1,0:T(8,128)(2,1)} %copy-done.7, f32[1,1024,768]{2,1,0:T(8,128)S(1)} %copy-done.2, f32[768]{0:T(1024)S(1)} %get-tuple-element.140, f32[768]{0:T(1024)S(1)} %get-tuple-element.141, f32[768]{0:T(1024)S(1)} %convert_element_type.209, f32[1024]{0:T(1024)S(1)} %fusion.87, ...), kind=kOutput, calls=%fused_computation.178 | convolution fusion | flops 4836556800 | bytes 18891776 | tf_op jit(solution)/shard_map/td,tf->df/dot_general | solution.py:202
  479.3 10.5 %fusion.78 = f32[3072,768]{1,0:T(8,128)} fusion(bf16[1024,3072]{1,0:T(8,128)(2,1)} %get-tuple-element.232, bf16[1,1024,768]{2,1,0:T(8,128)(2,1)S(1)} %copy-done.9, f32[768]{0:T(1024)S(1)} %get-tuple-element.139), kind=kOutput, calls=%fused_computation.129 | convolution fusion | flops 4834197504 | bytes 17304576 | tf_op jit(solution)/shard_map/tf,td->fd/dot_general | solution.py:193
  491.5 25.5 %reduce-scatter.6.cloned.1.call-done = f32[8,4608]{1,0:T(8,128)} async-done(((f32[128,4608]{1,0:T(8,128)}), f32[8,4608]{1,0:T(8,128)}) %reduce-scatter.6.cloned.1.call-update) | async-done | bytes 147472 | tf_op jit(solution)/shard_map/reduce_scatter | solution.py:265
  518.6 91.4 %reduce-scatter.8.cloned.1.call-done = f32[48,2304]{1,0:T(8,128)} async-done(((f32[768,2304]{1,0:T(8,128)}), f32[48,2304]{1,0:T(8,128)}) %reduce-scatter.8.cloned.1.call-update) | async-done | bytes 442384 | tf_op jit(solution)/shard_map/reduce_scatter | solution.py:268
  611.7 113.3 %reduce-scatter.12.cloned.1.call-done = f32[48,3072]{1,0:T(8,128)} async-done(((f32[768,3072]{1,0:T(8,128)}), f32[48,3072]{1,0:T(8,128)}) %reduce-scatter.12.cloned.1.call-update) | async-done | bytes 589840 | tf_op jit(solution)/shard_map/reduce_scatter | solution.py:271
  726.8 113.0 %reduce-scatter.14.cloned.1.call-done = f32[192,768]{1,0:T(8,128)} async-done(((f32[3072,768]{1,0:T(8,128)}), f32[192,768]{1,0:T(8,128)}) %reduce-scatter.14.cloned.1.call-update) | async-done | bytes 589840 | tf_op jit(solution)/shard_map/reduce_scatter | solution.py:273
  843.9 60.3 %all-reduce.12 = (bf16[4608]{0:T(1024)(128)(2,1)S(1)}, bf16[768]{0:T(1024)(128)(2,1)S(1)}, bf16[768]{0:T(1024)(128)(2,1)S(1)}, bf16[3072]{0:T(1024)(128)(2,1)S(1...) all-reduce(f32[4608]{0:T(1024)S(1)} %reduce.32, ...), channel_id=3, replica_groups=mesh['dp'=2,'fsdp'=16] {'fsdp'}, use_global_device_ids=true, to_apply=%region_23.24.clone | all-reduce | flops 10752 | bytes 64512
  904.6 4.9 all-reduce.14
  (314 shorter events, 213.2 us)
Async XLA Ops:
  7.2 77.3 %copy-start.3 = (bf16[1,1024,768]{2,1,0:T(8,128)(2,1)S(1)}, bf16[1,1024,768]{2,1,0:T(8,128)(2,1)}, u32[]{:S(2)}) copy-start(bf16[1,1024,768]{2,1,0:T(8,128)(2,1)} %param.20) | copy-start | bytes 4718596
  7.2 78.8 %copy-start.29 = (s32[1,1024]{1,0:T(1,128)S(1)}, s32[1,1024]{1,0:T(1,128)}, u32[]{:S(2)}) copy-start(s32[1,1024]{1,0:T(1,128)} %param.23) | copy-start | bytes 12292
  7.2 82.6 %all-gather.6.cloned.1.call-start = ((), (), s32[]{:S(2)}) async-start(), calls=%async_computation.5 | async-start | bytes 1253376 | tf_op jit(solution)/shard_map/all_gather | solution.py:92
  7.9 92.2 %all-gather.8.cloned.1.call-start = ((), (), s32[]{:S(2)}) async-start(), calls=%async_computation.6 | async-start | bytes 3760128 | tf_op jit(solution)/shard_map/all_gather | solution.py:95
  8.7 180.8 %all-gather.10.cloned.1.call-start = ((), (), s32[]{:S(2)}) async-start(), calls=%async_computation.7 | async-start | bytes 1253376 | tf_op jit(solution)/shard_map/all_gather | solution.py:96
  9.4 187.9 %all-gather.12.cloned.1.call-start = ((), (), s32[]{:S(2)}) async-start(), calls=%async_computation.8 | async-start | bytes 5013504 | tf_op jit(solution)/shard_map/all_gather | solution.py:98
  10.0 237.4 %all-gather.14.cloned.1.call-start = ((), (), s32[]{:S(2)}) async-start(), calls=%async_computation.9 | async-start | bytes 5013504 | tf_op jit(solution)/shard_map/all_gather | solution.py:100
  10.6 479.3 %reduce-scatter.10.cloned.1.call-start = ((), (), s32[]{:S(2)}) async-start(), calls=%async_computation.12 | async-start | bytes 2506752 | tf_op jit(solution)/shard_map/reduce_scatter | solution.py:269
  84.5 4.2 copy-start.32
  85.1 20.8 %copy-start.19 = (f32[1024]{0:T(1024)}, f32[1024]{0:T(1024)S(1)}, u32[]{:S(2)}) copy-start(f32[1024]{0:T(1024)S(1)} %broadcast_multiply_fusion.2) | copy-start | bytes 12292
  85.9 3.3 copy-start.21
  85.9 19.9 %copy-start.23 = (f32[1024]{0:T(1024)}, f32[1024]{0:T(1024)S(1)}, u32[]{:S(2)}) copy-start(f32[1024]{0:T(1024)S(1)} %fusion.86) | copy-start | bytes 12292
  86.0 19.9 %copy-start.25 = (f32[768]{0:T(1024)}, f32[768]{0:T(1024)S(1)}, u32[]{:S(2)}) copy-start(f32[768]{0:T(1024)S(1)} %convert_element_type.202) | copy-start | bytes 9220
  89.8 24.6 %copy-start.15 = (f32[1024,32]{0,1:T(8,128)}, f32[1024,32]{0,1:T(8,128)S(1)}, u32[]{:S(2)}) copy-start(f32[1024,32]{0,1:T(8,128)S(1)} %get-tuple-element.227) | copy-start | bytes 393220
  89.8 24.6 %copy-start.17 = (f32[1024,32]{0,1:T(8,128)}, f32[1024,32]{0,1:T(8,128)S(1)}, u32[]{:S(2)}) copy-start(f32[1024,32]{0,1:T(8,128)S(1)} %get-tuple-element.228) | copy-start | bytes 393220
  91.5 14.4 %copy-start.27 = (f32[768]{0:T(1024)}, f32[768]{0:T(1024)S(1)}, u32[]{:S(2)}) copy-start(f32[768]{0:T(1024)S(1)} %get-tuple-element.143) | copy-start | bytes 9220
  91.5 14.4 %copy-start.30 = (f32[768]{0:T(1024)}, f32[768]{0:T(1024)S(1)}, u32[]{:S(2)}) copy-start(f32[768]{0:T(1024)S(1)} %get-tuple-element.142) | copy-start | bytes 9220
  195.1 1.7 copy-start
  247.4 16.8 %copy-start.1 = (f32[1,1024,768]{2,1,0:T(8,128)S(1)}, f32[1,1024,768]{2,1,0:T(8,128)}, u32[]{:S(2)}) copy-start(f32[1,1024,768]{2,1,0:T(8,128)} %copy-done) | copy-start | bytes 9437188
  247.4 16.8 %copy-start.36 = (bf16[768,3072]{1,0:T(8,128)(2,1)S(1)}, bf16[768,3072]{1,0:T(8,128)(2,1)}, u32[]{:S(2)}) copy-start(bf16[768,3072]{1,0:T(8,128)(2,1)} %all-gather.12.cloned.1.call-done) | copy-start | bytes 14155780
  264.1 5.9 copy-start.7
  264.2 5.9 copy-start.8
  264.2 5.9 copy-start.35
  270.1 10.2 %copy-start.13 = (f32[1024,768]{1,0:T(8,128)}, f32[1024,768]{1,0:T(8,128)S(1)}, u32[]{:S(2)}) copy-start(f32[1024,768]{1,0:T(8,128)S(1)} %get-tuple-element.234) | copy-start | bytes 9437188
  280.7 1.7 copy-start.5
  286.6 230.4 %reduce-scatter.6.cloned.1.call-start = ((), (), s32[]{:S(2)}) async-start(), calls=%async_computation.10 | async-start | bytes 2506752 | tf_op jit(solution)/shard_map/reduce_scatter | solution.py:265
  296.0 131.9 %copy-start.16 = (f32[1024,32]{0,1:T(8,128)S(1)}, f32[1024,32]{0,1:T(8,128)}, u32[]{:S(2)}) copy-start(f32[1024,32]{0,1:T(8,128)} %copy-done.15) | copy-start | bytes 393220
  296.0 131.9 %copy-start.18 = (f32[1024,32]{0,1:T(8,128)S(1)}, f32[1024,32]{0,1:T(8,128)}, u32[]{:S(2)}) copy-start(f32[1024,32]{0,1:T(8,128)} %copy-done.17) | copy-start | bytes 393220
  432.0 4.0 copy-start.4
  432.0 4.0 copy-start.12
  432.1 4.0 copy-start.20
  432.1 4.0 copy-start.24
  432.1 4.0 copy-start.26
  432.1 4.0 copy-start.28
  433.9 2.1 copy-start.10
  442.8 4.3 copy-start.22
  447.1 3.3 copy-start.6
  447.1 3.8 copy-start.14
  450.9 2.4 copy-start.34
  453.2 2.0 copy-start.31
  455.0 155.0 %reduce-scatter.8.cloned.1.call-start = ((), (), s32[]{:S(2)}) async-start(), calls=%async_computation.11 | async-start | bytes 7520256 | tf_op jit(solution)/shard_map/reduce_scatter | solution.py:268
  465.1 2.0 copy-start.2
  465.1 259.9 %reduce-scatter.12.cloned.1.call-start = ((), (), s32[]{:S(2)}) async-start(), calls=%async_computation.13 | async-start | bytes 10027008 | tf_op jit(solution)/shard_map/reduce_scatter | solution.py:271
  477.9 1.4 copy-start.9
  477.9 361.8 %reduce-scatter.14.cloned.1.call-start = ((), (), s32[]{:S(2)}) async-start(), calls=%async_computation.14 | async-start | bytes 10027008 | tf_op jit(solution)/shard_map/reduce_scatter | solution.py:273
  489.8 423.0 %copy-start.11 = (bf16[128,4608]{1,0:T(8,128)(2,1)S(1)}, bf16[128,4608]{1,0:T(8,128)(2,1)}, u32[]{:S(2)}) copy-start(bf16[128,4608]{1,0:T(8,128)(2,1)} %all-gather.6.cloned.1.call-done) | copy-start | bytes 3538948
  489.8 423.0 %copy-start.33 = (bf16[1,128]{1,0:T(2,128)(2,1)S(1)}, bf16[1,128]{1,0:T(2,128)(2,1)}, u32[]{:S(2)}) copy-start(bf16[1,128]{1,0:T(2,128)(2,1)} %param.21) | copy-start | bytes 772
  489.8 424.5 %all-reduce.18.cloned.1.call-start = ((), (), s32[]{:S(2)}) async-start(), calls=%async_computation.15 | async-start | bytes 1916928 | tf_op jit(solution)/shard_map/psum | solution.py:278
Sparse Core Ops, SparseCore 0:
  10.3 41.2 all-gather.5
  53.8 46.2 all-gather.7
  102.4 36.9 all-gather.9
  141.5 51.9 all-gather.11
  195.7 51.6 all-gather.13
  286.7 61.7 reduce-scatter.9
  455.1 61.8 reduce-scatter.5
  521.0 88.9 reduce-scatter.7
  614.1 110.8 reduce-scatter.11
  728.9 110.7 reduce-scatter.13
  843.5 37.8 all-reduce.17
where the time goes:
time: 941 us; the launch traced here: 929 us
  waiting for transfers between devices  390 us (41%)
  matrix products  278 us (30%)
  blocking collectives  129 us (14%)
  other arithmetic  69.6 us (7%)
  local copies, waits for them, and re-layouts  43 us (5%)
  between operations  18.6 us (2%)
    unnamed x2, blocking collectives  124 us
    reduce_scatter x1, waiting for transfers between devices, shards(): lax.psum_scatter(grad_expander, 'fsdp', scatter_dimension=0, tiled=True)  113 us
    reduce_scatter x1, waiting for transfers between devices, shards(): lax.psum_scatter(grad_contractor, 'fsdp', scatter_dimension=0, tiled=True)  113 us
    reduce_scatter x1, waiting for transfers between devices, shards(): lax.psum_scatter(grad_projector, 'fsdp', scatter_dimension=0, tiled=True)  91.4 us
    dot_general x24, matrix products, head_scores(): jnp.einsum('sqd,skd->sqk', queries, keys, preferred_element_type=jnp.floa...  39.9 us
    all_gather x1, waiting for transfers between devices, shards(): lax.all_gather(contractor, 'fsdp', axis=0, tiled=True)  35.2 us
    dot_general x12, matrix products, attend_head(): jnp.einsum('sqk,skd->sqd', probs, values, preferred_element_type=jnp.floa...  31.3 us
    dot_general x12, matrix products, head_grads(): jnp.einsum('sqk,sqd->skd', probs.astype(jnp.bfloat16), upstream, preferre...  29.7 us
  transfers between devices with their start and end apart: 11, of which 6 were waited for; matrix products, arithmetic and copies ran while one was open for 36% of the time, Pallas kernels for 0%

commit v1 on v0

--- a/solution.py
+++ b/solution.py
@@ -6,6 +6,27 @@
 D = 768
 HEADS = 12
 HD = 64
+
+
+def collect(shard, axis, dim):
+    size, index, span = (lax.axis_size(axis), lax.axis_index(axis), shard.shape[dim])
+    forward = [(i, (i + 1) % size) for i in range(size)]
+    downward = [(i, (i - 1) % size) for i in range(size)]
+    out = jnp.zeros((*shard.shape[:dim], size * span, *shard.shape[dim + 1 :]), shard.dtype)
+    out = lax.dynamic_update_slice_in_dim(out, shard, index * span, axis=dim)
+    from_left = from_right = shard
+    half = size // 2
+    for step in range(1, half + 1):
+        from_left = lax.ppermute(from_left, axis, forward)
+        out = lax.dynamic_update_slice_in_dim(
+            out, from_left, (index - step) % size * span, axis=dim
+        )
+        if step < size - half:
+            from_right = lax.ppermute(from_right, axis, downward)
+            out = lax.dynamic_update_slice_in_dim(
+                out, from_right, (index + step) % size * span, axis=dim
+            )
+    return out
 
 
 def norm_shift(values, gain, shift, scale):
@@ -97,7 +118,7 @@
         lax.all_gather(midscale, "fsdp", axis=0, tiled=True),
         lax.all_gather(expander, "fsdp", axis=0, tiled=True),
         lax.all_gather(thresholds, "fsdp", axis=0, tiled=True),
-        lax.all_gather(contractor, "fsdp", axis=0, tiled=True),
+        collect(contractor, "fsdp", 0),
         lax.all_gather(baseline, "fsdp", axis=0, tiled=True),
         lax.all_gather(absorber, "fsdp", axis=0, tiled=True),
     )

time: 941 us -> 961 us (1.021)
  starting transfers between devices: 0.61 us -> 33.9 us
  waiting for transfers between devices: 390 us -> 365 us
  local copies, waits for them, and re-layouts: 43 us -> 55.2 us
    all_gather x1, waiting for transfers between devices: 35.2 us -> 0.01 us  [shards(): lax.all_gather(contractor, 'fsdp', axis=0, tiled=True)]
    ppermute x0 -> x15, starting transfers between devices: none -> 33.2 us  [the longest x7 32.6 us: collect(): from_right = lax.ppermute(from_right, axis, downward)]
    ppermute x0 -> x15, waiting for transfers between devices: none -> 20.5 us  [the longest x7 13.3 us: collect(): from_right = lax.ppermute(from_right, axis, downward)]
    dynamic_update_slice x0 -> x16, local copies, waits for them, and re-layouts: none -> 11.7 us  [the longest x8 5.86 us: collect(): lax.dynamic_update_slice_in_dim(out, from_left, (index - step) % size * s...]
  transfers between devices with their start and end apart: 11 -> 26, of which waited for: 6 -> 15; matrix products, arithmetic and copies ran while one was open for 36% -> 37% of each run, Pallas kernels for 0% -> 0%
where the time goes in v1:
time: 961 us; the launch traced here: 952 us
  waiting for transfers between devices  365 us (38%)
  matrix products  280 us (29%)
  blocking collectives  124 us (13%)
  other arithmetic  74.1 us (8%)
  local copies, waits for them, and re-layouts  55.2 us (6%)
  starting transfers between devices  33.9 us (4%)
  between operations  19 us (2%)
    unnamed x2, blocking collectives  119 us
    reduce_scatter x1, waiting for transfers between devices, shards(): lax.psum_scatter(grad_expander, 'fsdp', scatter_dimension=0, tiled=True)  113 us
    reduce_scatter x1, waiting for transfers between devices, shards(): lax.psum_scatter(grad_contractor, 'fsdp', scatter_dimension=0, tiled=True)  113 us
    reduce_scatter x1, waiting for transfers between devices, shards(): lax.psum_scatter(grad_projector, 'fsdp', scatter_dimension=0, tiled=True)  91.3 us
    dot_general x24, matrix products, head_scores(): jnp.einsum('sqd,skd->sqk', queries, keys, preferred_element_type=jnp.floa...  40 us
    ppermute x7, starting transfers between devices, collect(): from_right = lax.ppermute(from_right, axis, downward)  32.6 us
    dot_general x12, matrix products, attend_head(): jnp.einsum('sqk,skd->sqd', probs, values, preferred_element_type=jnp.floa...  31.2 us
    dot_general x12, matrix products, head_grads(): jnp.einsum('sqk,sqd->skd', probs.astype(jnp.bfloat16), upstream, preferre...  29.7 us
  transfers between devices with their start and end apart: 26, of which 15 were waited for; matrix products, arithmetic and copies ran while one was open for 37% of the time, Pallas kernels for 0%

profile of v1, /device:TPU:0, one launch (start us, length us, event | category | flops | bytes accessed | tf_op | source)
XLA Modules:
  0.0 951.9 jit_solution(9550767468117868754)
XLA Ops:
  10.6 5.0 collective-permute-start.1
  24.1 58.8 %all-reduce.13 = (bf16[4608]{0:T(1024)(128)(2,1)S(1)}, bf16[768]{0:T(1024)(128)(2,1)S(1)}, bf16[768]{0:T(1024)(128)(2,1)S(1)}, bf16[768]{0:T(1024)(128)(2,1)S(1)...) all-reduce(bf16[4608]{0:T(1024)(128)(2,1)S(1)} %dynamic-update-slic, ...), channel_id=1, replica_groups=mesh['dp'=2,'fsdp'=16] {'fsdp'}, use_global_device_ids=true, to_apply=%add.1 | all-reduce | flops 10752 | bytes 43008
  88.4 2.8 copy.69
  91.3 4.5 collective-permute-start.3
  101.0 4.7 collective-permute-start.5
  109.9 4.6 collective-permute-start.7
  116.7 2.8 collective-permute-done.7
  119.5 4.6 collective-permute-start.9
  129.0 4.6 collective-permute-start.11
  135.8 3.7 collective-permute-done.11
  139.5 4.6 collective-permute-start.13
  151.2 3.9 collective-permute-done.14
  155.8 5.9 copy.43
  161.8 6.4 fusion.74
  173.6 3.1 copy.45
  176.7 4.1 copy.46
  180.8 4.3 copy.47
  185.0 60.4 %while.28 = (s32[]{:T(128)}, bf16[12,1,1024,64]{2,3,1,0:T(8,128)(2,1)}, f32[12,1,1024]{2,1,0:T(1,128)S(1)}, bf16[12,1,1024,64]{3,2,1,0:T(8,128)(2,1)S(1)}, bf16[...) while((s32[]{:T(128)}, bf16[12,1,1024,64]{2,3,1,0:T(8,128)(2,1)}, ...), condition=%wide.region_5.6_spmd.clone, body=%wide.region_2.5_spmd.sunk.clone | while | flops 277871616 | bytes 13674569 | solution.py:167
  187.5 2.6 fusion.157
  192.5 2.6 fusion.157
  197.5 2.6 fusion.157
  202.6 2.6 fusion.157
  227.7 2.6 fusion.157
  232.8 2.6 fusion.157
  237.8 2.6 fusion.157
  242.9 2.6 fusion.157
  245.5 5.6 fusion.102
  253.3 15.2 %multiply_convert_fusion.1 = (bf16[1024,3072]{1,0:T(8,128)(2,1)}, f32[1024,3072]{1,0:T(8,128)}) fusion(f32[3072]{0:T(1024)S(1)} %convert_element_type.211, bf16[768,3072]{1,0:T(8,128)(2,1)} %all-gather.12.cloned.1.call-done, f32[1,1024,768]{2,1,0:T(8,128)} %copy-done, f32[768]{0:T(1024)S(1)} %get-tuple-element.140, f32[768]{0:T(1024)S(1)} %get-tuple-element.141, ...), kind=kOutput, calls=%fused_computation.65 | convolution fusion | flops 4868014080 | bytes 26768384 | tf_op jit(solution)/shard_map/dot_general | solution.py:177
  268.5 16.7 %convert_reduce_fusion = (f32[3072]{0:T(1024)S(1)}, bf16[1024,3072]{1,0:T(8,128)(2,1)S(1)}) fusion(f32[1024,3072]{1,0:T(8,128)} %get-tuple-element.233, f32[3072]{0:T(1024)S(1)} %convert_element_type.211, bf16[3072,768]{1,0:T(8,128)(2,1)} %all-gather.14.cloned.1.call-done, bf16[1,1024,768]{2,1,0:T(8,128)(2,1)} %param.35, f32[768]{0:T(1024)S(1)} %get-tuple-element.139), kind=kOutput, calls=%fused_computation.64 | convolution fusion | flops 4906546176 | bytes 25193472 | tf_op jit(solution)/shard_map/td,fd->tf/dot_general | solution.py:217
  285.3 5.9 fusion.58
  291.2 10.7 %fusion.57 = (f32[768]{0:T(1024)S(1)}, bf16[1,1024,768]{2,1,0:T(8,128)(2,1)}, f32[1024]{0:T(1024)S(1)}, f32[1,1024,768]{2,1,0:T(8,128)S(1)}) fusion(bf16[1,1024,768]{2,1,0:T(8,128)(2,1)S(1)} %copy-done.6, f32[768]{0:T(1024)S(1)} %convert_element_type.213, f32[1,1024,768]{2,1,0:T(8,128)S(1)} %copy-done.1, f32[768]{0:T(1024)S(1)} %get-tuple-element.139, ...), kind=kOutput, calls=%fused_computation.73 | convolution fusion | flops 4843632640 | bytes 23624704 | tf_op jit(solution)/shard_map/dot_general | solution.py:181
  303.9 5.1 fusion.81
  309.2 4.8 convolution_convert_fusion
  313.9 4.4 copy.48
  318.3 131.9 %while.29 = (s32[]{:T(128)}, f32[12,1,1024,64]{2,3,1,0:T(8,128)}, f32[12,1,1024,64]{2,3,1,0:T(8,128)}, bf16[12,1,1024,64]{2,3,1,0:T(8,128)(2,1)}, bf16[12,1,1024...) while((s32[]{:T(128)}, f32[12,1,1024,64]{2,3,1,0:T(8,128)}, ...), condition=%wide.region_12.13_spmd.clone, body=%wide.region_10.12_spmd.sunk.clone | while | flops 683801600 | bytes 34112608 | solution.py:241
  450.2 3.9 multiply_add_fusion.1
  458.5 6.7 fusion.59
  469.5 3.2 fusion.100
  472.7 3.7 select_reduce_fusion
  478.6 9.8 %fusion.76 = f32[768,2304]{1,0:T(8,128)} fusion(bf16[1024,2304]{0,1:T(8,128)(2,1)} %bitcast.248, bf16[1,1024,768]{2,1,0:T(8,128)(2,1)S(1)} %copy-done.4, f32[768]{0:T(1024)S(1)} %copy-done.30, f32[768]{0:T(1024)S(1)} %copy-done.27, f32[768]{0:T(1024)S(1)} %copy-done.23, f32[1024]{0:T(1024)S(1)} %copy-done.25, f32[1024]{0:T(1024)S(1)} %copy-done.19, ...), kind=kOutput, calls=%fused_computation.118 | convolution fusion | flops 3630170112 | bytes 13390848 | tf_op jit(solution)/shard_map/td,te->de/dot_general | solution.py:252
  490.4 10.9 %fusion.96 = f32[768,3072]{1,0:T(8,128)} fusion(bf16[1024,3072]{1,0:T(8,128)(2,1)} %copy-done.5, f32[1,1024,768]{2,1,0:T(8,128)S(1)} %copy-done.2, f32[768]{0:T(1024)S(1)} %get-tuple-element.140, f32[768]{0:T(1024)S(1)} %get-tuple-element.141, f32[768]{0:T(1024)S(1)} %convert_element_type.209, f32[1024]{0:T(1024)S(1)} %fusion.87, ...), kind=kOutput, calls=%fused_computation.194 | convolution fusion | flops 4836556800 | bytes 18891776 | tf_op jit(solution)/shard_map/td,tf->df/dot_general | solution.py:223
  502.7 10.5 %fusion.78 = f32[3072,768]{1,0:T(8,128)} fusion(bf16[1024,3072]{1,0:T(8,128)(2,1)} %get-tuple-element.232, bf16[1,1024,768]{2,1,0:T(8,128)(2,1)S(1)} %copy-done.7, f32[768]{0:T(1024)S(1)} %get-tuple-element.139), kind=kOutput, calls=%fused_computation.129 | convolution fusion | flops 4834197504 | bytes 17304576 | tf_op jit(solution)/shard_map/tf,td->fd/dot_general | solution.py:214
  515.0 24.2 %reduce-scatter.6.cloned.1.call-done = f32[8,4608]{1,0:T(8,128)} async-done(((f32[128,4608]{1,0:T(8,128)}), f32[8,4608]{1,0:T(8,128)}) %reduce-scatter.6.cloned.1.call-update) | async-done | bytes 147472 | tf_op jit(solution)/shard_map/reduce_scatter | solution.py:286
  540.7 91.3 %reduce-scatter.8.cloned.1.call-done = f32[48,2304]{1,0:T(8,128)} async-done(((f32[768,2304]{1,0:T(8,128)}), f32[48,2304]{1,0:T(8,128)}) %reduce-scatter.8.cloned.1.call-update) | async-done | bytes 442384 | tf_op jit(solution)/shard_map/reduce_scatter | solution.py:289
  633.8 113.3 %reduce-scatter.12.cloned.1.call-done = f32[48,3072]{1,0:T(8,128)} async-done(((f32[768,3072]{1,0:T(8,128)}), f32[48,3072]{1,0:T(8,128)}) %reduce-scatter.12.cloned.1.call-update) | async-done | bytes 589840 | tf_op jit(solution)/shard_map/reduce_scatter | solution.py:292
  748.9 113.0 %reduce-scatter.14.cloned.1.call-done = f32[192,768]{1,0:T(8,128)} async-done(((f32[3072,768]{1,0:T(8,128)}), f32[192,768]{1,0:T(8,128)}) %reduce-scatter.14.cloned.1.call-update) | async-done | bytes 589840 | tf_op jit(solution)/shard_map/reduce_scatter | solution.py:294
  866.1 60.3 %all-reduce.12 = (bf16[4608]{0:T(1024)(128)(2,1)S(1)}, bf16[768]{0:T(1024)(128)(2,1)S(1)}, bf16[768]{0:T(1024)(128)(2,1)S(1)}, bf16[3072]{0:T(1024)(128)(2,1)S(1...) all-reduce(f32[4608]{0:T(1024)S(1)} %reduce.32, ...), channel_id=3, replica_groups=mesh['dp'=2,'fsdp'=16] {'fsdp'}, use_global_device_ids=true, to_apply=%region_23.24.clone | all-reduce | flops 10752 | bytes 64512
  926.8 4.9 all-reduce.14
  (359 shorter events, 259.2 us)
Async XLA Ops:
  7.2 78.3 %copy-start.3 = (bf16[1,1024,768]{2,1,0:T(8,128)(2,1)S(1)}, bf16[1,1024,768]{2,1,0:T(8,128)(2,1)}, u32[]{:S(2)}) copy-start(bf16[1,1024,768]{2,1,0:T(8,128)(2,1)} %param.20) | copy-start | bytes 4718596
  7.2 79.2 %copy-start.28 = (s32[1,1024]{1,0:T(1,128)S(1)}, s32[1,1024]{1,0:T(1,128)}, u32[]{:S(2)}) copy-start(s32[1,1024]{1,0:T(1,128)} %param.23) | copy-start | bytes 12292
  7.2 142.4 %all-gather.6.cloned.1.call-start = ((), (), s32[]{:S(2)}) async-start(), calls=%async_computation.5 | async-start | bytes 1253376 | tf_op jit(solution)/shard_map/all_gather | solution.py:113
  7.9 147.9 %all-gather.8.cloned.1.call-start = ((), (), s32[]{:S(2)}) async-start(), calls=%async_computation.6 | async-start | bytes 3760128 | tf_op jit(solution)/shard_map/all_gather | solution.py:116
  8.7 236.8 %all-gather.10.cloned.1.call-start = ((), (), s32[]{:S(2)}) async-start(), calls=%async_computation.7 | async-start | bytes 1253376 | tf_op jit(solution)/shard_map/all_gather | solution.py:117
  9.4 243.9 %all-gather.12.cloned.1.call-start = ((), (), s32[]{:S(2)}) async-start(), calls=%async_computation.8 | async-start | bytes 5013504 | tf_op jit(solution)/shard_map/all_gather | solution.py:119
  10.0 258.5 %all-gather.14.cloned.1.call-start = ((), (), s32[]{:S(2)}) async-start(), calls=%async_computation.9 | async-start | bytes 5013504 | tf_op jit(solution)/shard_map/all_gather | solution.py:193
  10.0 77.0 %collective-permute-start = (bf16[192,768]{1,0:T(8,128)(2,1)}, bf16[192,768]{1,0:T(8,128)(2,1)S(1)}, u32[]{:S(2)}, u32[]{:S(2)}) collective-permute-start(bf16[192,768]{1,0:T(8,128)(2,1)} %param.32), channel_id=1, source_target_pairs={{0,1},{1,2},{2,3},{3,4},{4,5},{5,6},{6,7},{7,8},{8,9},{9,10},{10,1... | collective-permute-start | bytes 884744 | tf_op jit(solution)/shard_map/ppermute | solution.py:20
  10.6 80.7 %collective-permute-start.1 = (bf16[192,768]{1,0:T(8,128)(2,1)}, bf16[192,768]{1,0:T(8,128)(2,1)S(1)}, u32[]{:S(2)}, u32[]{:S(2)}) collective-permute-start(bf16[192,768]{1,0:T(8,128)(2,1)} %param.32), channel_id=1, source_target_pairs={{0,15},{1,0},{2,1},{3,2},{4,3},{5,4},{6,5},{7,6},{8,7},{9,8},{10,9... | collective-permute-start | bytes 884744 | tf_op jit(solution)/shard_map/ppermute | solution.py:25
  15.7 497.7 %reduce-scatter.10.cloned.1.call-start = ((), (), s32[]{:S(2)}) async-start(), calls=%async_computation.12 | async-start | bytes 2506752 | tf_op jit(solution)/shard_map/reduce_scatter | solution.py:290
  85.5 76.2 %copy-start.18 = (f32[1024]{0:T(1024)}, f32[1024]{0:T(1024)S(1)}, u32[]{:S(2)}) copy-start(f32[1024]{0:T(1024)S(1)} %broadcast_multiply_fusion.2) | copy-start | bytes 12292
  86.4 13.7 %copy-start.20 = (f32[1024]{0:T(1024)}, f32[1024]{0:T(1024)S(1)}, u32[]{:S(2)}) copy-start(f32[1024]{0:T(1024)S(1)} %multiply_reduce_fusion.3) | copy-start | bytes 12292
  87.0 83.5 %copy-start.13 = (f32[1024,32]{0,1:T(8,128)}, f32[1024,32]{0,1:T(8,128)S(1)}, u32[]{:S(2)}) copy-start(f32[1024,32]{0,1:T(8,128)S(1)} %get-tuple-element.227) | copy-start | bytes 393220
  87.0 83.5 %copy-start.15 = (f32[1024,32]{0,1:T(8,128)}, f32[1024,32]{0,1:T(8,128)S(1)}, u32[]{:S(2)}) copy-start(f32[1024,32]{0,1:T(8,128)S(1)} %get-tuple-element.228) | copy-start | bytes 393220
  87.0 10.6 %collective-permute-start.2 = (bf16[192,768]{1,0:T(8,128)(2,1)S(1)}, bf16[192,768]{1,0:T(8,128)(2,1)S(1)}, u32[]{:S(2)}, u32[]{:S(2)}) collective-permute-start(bf16[192,768]{1,0:T(8,128)(2,1)S(1)} %collective-permute-done), channel_id=1, source_target_pairs={{0,1},{1,2},{2,3},{3,4},{4,5},{5,6},{6,7},{7,8},{8,9},{9,10},{10,1... | collective-permute-start | bytes 884744 | tf_op jit(solution)/shard_map/ppermute | solution.py:20
  88.4 73.3 %copy-start.22 = (f32[768]{0:T(1024)}, f32[768]{0:T(1024)S(1)}, u32[]{:S(2)}) copy-start(f32[768]{0:T(1024)S(1)} %convert_element_type.202) | copy-start | bytes 9220
  91.2 8.9 copy-start.17
  91.2 14.4 %copy-start.31 = (bf16[1,128]{1,0:T(2,128)(2,1)S(1)}, bf16[1,128]{1,0:T(2,128)(2,1)}, u32[]{:S(2)}) copy-start(bf16[1,128]{1,0:T(2,128)(2,1)} %param.21) | copy-start | bytes 772
  91.3 9.7 %collective-permute-start.3 = (bf16[192,768]{1,0:T(8,128)(2,1)S(1)}, bf16[192,768]{1,0:T(8,128)(2,1)S(1)}, u32[]{:S(2)}, u32[]{:S(2)}) collective-permute-start(bf16[192,768]{1,0:T(8,128)(2,1)S(1)} %collective-permute-done.1), channel_id=1, source_target_pairs={{0,15},{1,0},{2,1},{3,2},{4,3},{5,4},{6,5},{7,6},{8,7},{9,8},{10,9... | collective-permute-start | bytes 884744 | tf_op jit(solution)/shard_map/ppermute | solution.py:25
  95.8 66.0 %copy-start.24 = (f32[1024]{0:T(1024)}, f32[1024]{0:T(1024)S(1)}, u32[]{:S(2)}) copy-start(f32[1024]{0:T(1024)S(1)} %fusion.86) | copy-start | bytes 12292
  97.6 9.1 collective-permute-start.4
  101.0 8.9 collective-permute-start.5
  106.8 9.2 collective-permute-start.6
  109.9 9.6 %collective-permute-start.7 = (bf16[192,768]{1,0:T(8,128)(2,1)S(1)}, bf16[192,768]{1,0:T(8,128)(2,1)S(1)}, u32[]{:S(2)}, u32[]{:S(2)}) collective-permute-start(bf16[192,768]{1,0:T(8,128)(2,1)S(1)} %collective-permute-done.5), channel_id=1, source_target_pairs={{0,15},{1,0},{2,1},{3,2},{4,3},{5,4},{6,5},{7,6},{8,7},{9,8},{10,9... | collective-permute-start | bytes 884744 | tf_op jit(solution)/shard_map/ppermute | solution.py:25
  116.0 9.7 %collective-permute-start.8 = (bf16[192,768]{1,0:T(8,128)(2,1)S(1)}, bf16[192,768]{1,0:T(8,128)(2,1)S(1)}, u32[]{:S(2)}, u32[]{:S(2)}) collective-permute-start(bf16[192,768]{1,0:T(8,128)(2,1)S(1)} %collective-permute-done.6), channel_id=1, source_target_pairs={{0,1},{1,2},{2,3},{3,4},{4,5},{5,6},{6,7},{7,8},{8,9},{9,10},{10,1... | collective-permute-start | bytes 884744 | tf_op jit(solution)/shard_map/ppermute | solution.py:20
  119.5 9.5 collective-permute-start.9
  125.7 9.3 collective-permute-start.10
  129.0 10.5 %collective-permute-start.11 = (bf16[192,768]{1,0:T(8,128)(2,1)S(1)}, bf16[192,768]{1,0:T(8,128)(2,1)S(1)}, u32[]{:S(2)}, u32[]{:S(2)}) collective-permute-start(bf16[192,768]{1,0:T(8,128)(2,1)S(1)} %collective-permute-done.9), channel_id=1, source_target_pairs={{0,15},{1,0},{2,1},{3,2},{4,3},{5,4},{6,5},{7,6},{8,7},{9,8},{10,9... | collective-permute-start | bytes 884744 | tf_op jit(solution)/shard_map/ppermute | solution.py:25
  135.0 11.2 %collective-permute-start.12 = (bf16[192,768]{1,0:T(8,128)(2,1)S(1)}, bf16[192,768]{1,0:T(8,128)(2,1)S(1)}, u32[]{:S(2)}, u32[]{:S(2)}) collective-permute-start(bf16[192,768]{1,0:T(8,128)(2,1)S(1)} %collective-permute-done.10), channel_id=1, source_target_pairs={{0,1},{1,2},{2,3},{3,4},{4,5},{5,6},{6,7},{7,8},{8,9},{9,10},{10,1... | collective-permute-start | bytes 884744 | tf_op jit(solution)/shard_map/ppermute | solution.py:20
  139.5 9.3 collective-permute-start.13
  146.3 8.8 collective-permute-start.14
  151.2 10.6 %copy-start.26 = (f32[768]{0:T(1024)}, f32[768]{0:T(1024)S(1)}, u32[]{:S(2)}) copy-start(f32[768]{0:T(1024)S(1)} %get-tuple-element.143) | copy-start | bytes 9220
  151.2 10.6 %copy-start.29 = (f32[768]{0:T(1024)}, f32[768]{0:T(1024)S(1)}, u32[]{:S(2)}) copy-start(f32[768]{0:T(1024)S(1)} %get-tuple-element.142) | copy-start | bytes 9220
  268.5 16.7 %copy-start.1 = (f32[1,1024,768]{2,1,0:T(8,128)S(1)}, f32[1,1024,768]{2,1,0:T(8,128)}, u32[]{:S(2)}) copy-start(f32[1,1024,768]{2,1,0:T(8,128)} %copy-done) | copy-start | bytes 9437188
  268.5 16.7 %copy-start.34 = (bf16[768,3072]{1,0:T(8,128)(2,1)S(1)}, bf16[768,3072]{1,0:T(8,128)(2,1)}, u32[]{:S(2)}) copy-start(bf16[768,3072]{1,0:T(8,128)(2,1)} %all-gather.12.cloned.1.call-done) | copy-start | bytes 14155780
  285.2 5.9 copy-start.5
  285.2 6.0 copy-start.6
  285.3 6.0 copy-start.35
  291.2 10.7 %copy-start.11 = (f32[1024,768]{1,0:T(8,128)}, f32[1024,768]{1,0:T(8,128)S(1)}, u32[]{:S(2)}) copy-start(f32[1024,768]{1,0:T(8,128)S(1)} %get-tuple-element.234) | copy-start | bytes 9437188
  309.1 230.1 %reduce-scatter.6.cloned.1.call-start = ((), (), s32[]{:S(2)}) async-start(), calls=%async_computation.10 | async-start | bytes 2506752 | tf_op jit(solution)/shard_map/reduce_scatter | solution.py:286
  318.3 131.9 %copy-start.14 = (f32[1024,32]{0,1:T(8,128)S(1)}, f32[1024,32]{0,1:T(8,128)}, u32[]{:S(2)}) copy-start(f32[1024,32]{0,1:T(8,128)} %copy-done.13) | copy-start | bytes 393220
  318.3 131.9 %copy-start.16 = (f32[1024,32]{0,1:T(8,128)S(1)}, f32[1024,32]{0,1:T(8,128)}, u32[]{:S(2)}) copy-start(f32[1024,32]{0,1:T(8,128)} %copy-done.15) | copy-start | bytes 393220
  478.3 153.8 %reduce-scatter.8.cloned.1.call-start = ((), (), s32[]{:S(2)}) async-start(), calls=%async_computation.11 | async-start | bytes 7520256 | tf_op jit(solution)/shard_map/reduce_scatter | solution.py:289
  488.5 258.6 %reduce-scatter.12.cloned.1.call-start = ((), (), s32[]{:S(2)}) async-start(), calls=%async_computation.13 | async-start | bytes 10027008 | tf_op jit(solution)/shard_map/reduce_scatter | solution.py:292
  501.3 360.6 %reduce-scatter.14.cloned.1.call-start = ((), (), s32[]{:S(2)}) async-start(), calls=%async_computation.14 | async-start | bytes 10027008 | tf_op jit(solution)/shard_map/reduce_scatter | solution.py:294
  513.3 421.7 %copy-start.9 = (bf16[128,4608]{1,0:T(8,128)(2,1)S(1)}, bf16[128,4608]{1,0:T(8,128)(2,1)}, u32[]{:S(2)}) copy-start(bf16[128,4608]{1,0:T(8,128)(2,1)} %all-gather.6.cloned.1.call-done) | copy-start | bytes 3538948
  513.3 421.7 %copy-start.32 = (bf16[1,128]{1,0:T(2,128)(2,1)S(1)}, bf16[1,128]{1,0:T(2,128)(2,1)}, u32[]{:S(2)}) copy-start(bf16[1,128]{1,0:T(2,128)(2,1)} %param.21) | copy-start | bytes 772
  513.3 423.2 %all-reduce.18.cloned.1.call-start = ((), (), s32[]{:S(2)}) async-start(), calls=%async_computation.15 | async-start | bytes 1916928 | tf_op jit(solution)/shard_map/psum | solution.py:299
  (14 other events, 44.8 us)
Sparse Core Ops, SparseCore 0:
  10.3 41.1 all-gather.5
  53.8 55.2 all-gather.7
  111.3 41.8 all-gather.9
  155.4 51.8 all-gather.11
  209.5 51.6 all-gather.13
  309.2 60.8 reduce-scatter.9
  478.4 60.7 reduce-scatter.5
  543.2 88.8 reduce-scatter.7
  636.2 110.8 reduce-scatter.11
  751.1 110.8 reduce-scatter.13
  865.7 37.8 all-reduce.17
